TPU v7x, 32 devices: a whole 2x2x4 slice. The times are simulated.
32 devices in a mesh: row: 8 (over y, x, core), shift: 4 (over z).
Axes of the slice: x: 2, y: 2, z: 4, core: 2. Of those that a mesh axis runs over, the one named last changes fastest.
Arguments:
- snapshots: bfloat16 [4096, 2, 128], P('row'), may hold values from -6 to 6
- tail_sensors: bfloat16 [128, 2, 128], replicated, may hold values from -6 to 6
- shift_offsets: int32 [12], P('shift'), may hold values from 0 to 128
- start_basis: float32 [64, 4096], P(None, 'row'), may hold values from -0.09375 to 0.09375
Outputs:
- covariance: float32 [4096, 4096], P('row', 'shift')
- signal_basis: float32 [64, 4096], P(None, 'row')
Inputs may be any that keep to these rules, and one draw needn't show every extreme that they name: `shift_offsets`: each shift's first sensor.
All inputs are finite; a program needn't handle non-finite values.
Results may differ from a plain program's by a relative error of at most 0.0031.
Values may be sent and summed in bfloat16 or wider, within the bound.
A program may use at most 64 MiB of HBM per device.

v0:
```python
import jax
import jax.numpy as jnp
from jax import lax
from jax.sharding import PartitionSpec as P

M = 4096
SNAPS = 128
ITERS = 2
half_root = 0.7071067811865476


def make_some(extended, offset, start, count):
    window = lax.dynamic_slice_in_dim(extended, offset + start, count, 0).astype(jnp.float32)
    mirror = lax.dynamic_slice_in_dim(extended, offset + M - start - count, count, 0).astype(
        jnp.float32
    )[::-1]
    summed_pair = window + mirror
    difference = window - mirror
    upper_rows = jnp.concatenate([summed_pair[:, 0], summed_pair[:, 1]], axis=1)
    bottom = jnp.concatenate([difference[:, 1], -difference[:, 0]], axis=1)
    positions = start + jnp.arange(count, dtype=jnp.int32)
    chosen = jnp.where((positions < M // 2)[:, None], upper_rows, bottom)
    return (chosen * half_root).astype(jnp.bfloat16)


def factor(gram_matrix):
    lower_factor = jnp.linalg.cholesky(gram_matrix)
    identity = jnp.eye(gram_matrix.shape[0], dtype=jnp.float32)
    return jax.scipy.linalg.solve_triangular(lower_factor, identity, lower=True)


def per_device(snapshots, tail_sensors, shift_offsets, start_basis):
    block_rows = snapshots.shape[0]
    row_index = lax.axis_index("row")
    shift_index = lax.axis_index("shift")
    col_count = M // lax.axis_size("shift")
    normalizer = 1.0 / (SNAPS * shift_offsets.shape[0] * lax.axis_size("shift"))
    gathered = lax.all_gather(snapshots, "row", axis=0, tiled=True)
    extended = jnp.concatenate([gathered, tail_sensors], 0)
    every_offset = lax.all_gather(shift_offsets, "shift", axis=0, tiled=True)
    row_start = row_index * block_rows
    col_start = shift_index * col_count

    def add_block(which, running):
        offset = every_offset[which]
        own_rows = make_some(extended, offset, row_start, block_rows)
        col_rows = make_some(extended, offset, col_start, col_count)
        return running + lax.dot_general(
            own_rows, col_rows, (((1,), (1,)), ((), ())), preferred_element_type=jnp.float32
        )

    summed_block = lax.fori_loop(
        0, every_offset.shape[0], add_block, jnp.zeros((block_rows, col_count), jnp.float32)
    )
    cov_out = summed_block * normalizer
    basis_rows = lax.all_gather(start_basis, "row", axis=1, tiled=True)
    own_basis = start_basis
    for sweep in range(ITERS):
        basis_cols = lax.dynamic_slice_in_dim(basis_rows, shift_index * col_count, col_count, 1)
        column_terms = lax.dot_general(
            basis_cols, cov_out, (((1,), (1,)), ((), ())), precision=lax.Precision.HIGHEST
        )
        mapped = lax.psum(column_terms, "shift")
        local_gram = jnp.dot(mapped, mapped.T, precision=lax.Precision.HIGHEST)
        gram_matrix = lax.psum(local_gram, "row")
        own_basis = jnp.dot(factor(gram_matrix), mapped, precision=lax.Precision.HIGHEST)
        if sweep + 1 < ITERS:
            basis_rows = lax.all_gather(own_basis, "row", axis=1, tiled=True)
    return (cov_out, own_basis)


def solution(mesh):
    in_specs = (P("row", None, None), P(), P("shift"), P(None, "row"))
    out_specs = (P("row", "shift"), P(None, "row"))
    return jax.shard_map(
        per_device, mesh=mesh, in_specs=in_specs, out_specs=out_specs, check_vma=False
    )
```

profile of v0, /device:TPU:0, one launch (start us, length us, event | category | flops | bytes accessed | tf_op | source)
XLA Modules:
  0.0 375.3 jit_solution(9196168970584460465)
XLA Ops:
  8.7 1.3 dynamic-slice
  11.5 9.9 %all-reduce = s32[12]{0:T(128)S(1)} all-reduce(s32[12]{0:T(128)S(1)} %dynamic-update-slice.2), channel_id=1, replica_groups=mesh['row'=8,'shift'=4] {'shift'}, use_global_device_ids=true, to_apply=%add | all-reduce | flops 12 | bytes 96
  21.4 19.0 %all-gather.4.cloned.1.call-done = bf16[4096,2,128]{2,1,0:T(2,128)(2,1)} async-done(((bf16[512,2,128]{2,1,0:T(2,128)(2,1)}), bf16[4096,2,128]{2,1,0:T(2,128)(2,1)}) %all-gather.4.cloned.1.call-update) | async-done | bytes 2097168 | tf_op jit(solution)/shard_map/all_gather | solution.py:38
  40.4 6.4 %pad_maximum_fusion = bf16[4224,2,128]{2,1,0:T(2,128)(2,1)S(1)} fusion(bf16[128,2,128]{2,1,0:T(2,128)(2,1)} %param.10, bf16[4096,2,128]{2,1,0:T(2,128)(2,1)} %all-gather.4.cloned.1.call-done), kind=kLoop, calls=%fused_computation.31 | loop fusion | flops 1081344 | bytes 4325376 | tf_op jit(solution)/shard_map/concatenate | solution.py:39
  46.8 1.6 copy.30
  48.4 143.1 %while.18 = (s32[]{:T(128)}, f32[512,1024]{1,0:T(8,128)}, s32[]{:T(128)}, s32[12]{0:T(128)S(1)}, bf16[4224,2,128]{2,0,1:T(8,128)(2,1)}, /*index=5*/s32[]{:T(128)...) while((s32[]{:T(128)}, f32[512,1024]{1,0:T(8,128)}, ...), condition=%wide.region_1.2_spmd.clone, body=%wide.region_0.1_spmd.clone.sunk | while | flops 273222688 | bytes 47713820 | solution.py:52
  49.7 1.2 dynamic-slice_convert_fusion.4
  52.0 1.2 convert_subtract_fusion.4
  53.2 1.2 slice_bitcast_fusion.8
  56.5 1.2 convert_subtract_fusion.5
  59.1 1.3 copy-done.1
  63.9 1.2 convert_subtract_fusion.4
  65.2 1.2 slice_bitcast_fusion.8
  68.4 1.2 convert_subtract_fusion.5
  71.0 1.3 copy-done.1
  75.8 1.2 convert_subtract_fusion.4
  77.1 1.2 slice_bitcast_fusion.8
  80.4 1.2 convert_subtract_fusion.5
  82.9 1.3 copy-done.1
  87.8 1.2 convert_subtract_fusion.4
  89.0 1.2 slice_bitcast_fusion.8
  92.3 1.2 convert_subtract_fusion.5
  94.9 1.3 copy-done.1
  99.7 1.2 convert_subtract_fusion.4
  100.9 1.2 slice_bitcast_fusion.8
  104.2 1.2 convert_subtract_fusion.5
  106.8 1.3 copy-done.1
  111.6 1.2 convert_subtract_fusion.4
  112.9 1.2 slice_bitcast_fusion.8
  118.7 1.3 copy-done.1
  123.5 1.2 convert_subtract_fusion.4
  124.8 1.2 slice_bitcast_fusion.8
  130.6 1.3 copy-done.1
  135.5 1.2 convert_subtract_fusion.4
  136.7 1.2 slice_bitcast_fusion.8
  142.6 1.3 copy-done.1
  147.4 1.2 convert_subtract_fusion.4
  148.6 1.2 slice_bitcast_fusion.8
  154.5 1.3 copy-done.1
  159.3 1.2 convert_subtract_fusion.4
  160.6 1.2 slice_bitcast_fusion.8
  166.4 1.3 copy-done.1
  171.2 1.2 convert_subtract_fusion.4
  172.5 1.2 slice_bitcast_fusion.8
  178.3 1.3 copy-done.1
  183.2 1.2 convert_subtract_fusion.4
  184.4 1.2 slice_bitcast_fusion.8
  190.3 1.3 copy-done.1
  191.6 1.8 broadcast_multiply_fusion
  193.4 4.0 %fusion.16 = f32[64,512]{1,0:T(8,128)} fusion(f32[512,1024]{1,0:T(8,128)S(1)} %broadcast_multiply_fusion, f32[64,4096]{1,0:T(8,128)} %all-gather.6.cloned.1.call-done, s32[]{:T(128)S(6)} %select_n.96), kind=kOutput, calls=%fused_computation.35 | convolution fusion | flops 402653184 | bytes 2490372 | tf_op jit(solution)/shard_map/dot_general | solution.py:60
  197.5 34.7 %all-reduce.4.cloned.1.call-done = f32[64,512]{1,0:T(8,128)} async-done(((f32[64,512]{1,0:T(8,128)}), f32[64,512]{1,0:T(8,128)}) %all-reduce.4.cloned.1.call-update) | async-done | bytes 131088 | tf_op jit(solution)/shard_map/psum | solution.py:63
  232.2 1.2 fusion.32
  233.4 22.4 %psum.29 = f32[64,64]{0,1:T(8,128)S(1)} all-reduce(f32[64,64]{0,1:T(8,128)S(1)} %fusion.32), channel_id=1, replica_groups=mesh['row'=8,'shift'=4] {'row'}, use_global_device_ids=true, to_apply=%region_3.4 | all-reduce | flops 4096 | bytes 32768 | tf_op jit(solution)/shard_map/psum | solution.py:65
  255.9 5.8 %cholesky.44 = f32[64,64]{1,0:T(8,128)S(1)} custom-call(f32[64,64]{1,0:T(8,128)S(1)} %fusion.27), custom_call_target="Cholesky" | custom-call | tf_op jit(solution)/shard_map/jit(cholesky)/cholesky | solution.py:27
  263.1 4.9 %custom-call.7 = f32[1,64,64]{1,2,0:T(8,128)S(1)} custom-call(f32[1,64,64]{2,1,0:T(8,128)S(1)} %fusion.22), custom_call_target="InvertDiagBlocksLowerTriangular" | custom-call | tf_op jit(solution)/shard_map/jit(_solve_triangular)/triangular_solve | solution.py:29
  268.2 1.8 fusion.33
  270.1 22.3 %all-gather.8.cloned.1.call-done = f32[64,4096]{1,0:T(8,128)} async-done(((f32[64,512]{1,0:T(8,128)}), f32[64,4096]{1,0:T(8,128)}) %all-gather.8.cloned.1.call-update) | async-done | bytes 1048592 | tf_op jit(solution)/shard_map/all_gather | solution.py:68
  292.4 3.7 fusion.14
  296.2 34.8 %all-reduce.6.cloned.1.call-done = f32[64,512]{1,0:T(8,128)} async-done(((f32[64,512]{1,0:T(8,128)}), f32[64,512]{1,0:T(8,128)}) %all-reduce.6.cloned.1.call-update) | async-done | bytes 131088 | tf_op jit(solution)/shard_map/psum | solution.py:63
  331.0 1.2 fusion.34
  332.2 22.4 %psum.31 = f32[64,64]{0,1:T(8,128)S(1)} all-reduce(f32[64,64]{0,1:T(8,128)S(1)} %fusion.34), channel_id=1, replica_groups=mesh['row'=8,'shift'=4] {'row'}, use_global_device_ids=true, to_apply=%region_7.10 | all-reduce | flops 4096 | bytes 32768 | tf_op jit(solution)/shard_map/psum | solution.py:65
  354.6 5.8 %cholesky.55 = f32[64,64]{1,0:T(8,128)S(1)} custom-call(f32[64,64]{1,0:T(8,128)S(1)} %fusion.25), custom_call_target="Cholesky" | custom-call | tf_op jit(solution)/shard_map/jit(cholesky)/cholesky | solution.py:27
  361.8 4.9 %custom-call.8 = f32[1,64,64]{1,2,0:T(8,128)S(1)} custom-call(f32[1,64,64]{2,1,0:T(8,128)S(1)} %fusion.23), custom_call_target="InvertDiagBlocksLowerTriangular" | custom-call | tf_op jit(solution)/shard_map/jit(_solve_triangular)/triangular_solve | solution.py:29
  367.0 1.8 fusion.35
  (250 shorter events, 71.0 us)
Async XLA Ops:
  7.2 33.2 %all-gather.4.cloned.1.call-start = ((), (), s32[]{:S(2)}) async-start(), calls=%async_computation | async-start | bytes 2359296 | tf_op jit(solution)/shard_map/all_gather | solution.py:38
  7.9 185.5 %all-gather.6.cloned.1.call-start = ((), (), s32[]{:S(2)}) async-start(), calls=%async_computation.1 | async-start | bytes 1179648 | tf_op jit(solution)/shard_map/all_gather | solution.py:56
  8.6 223.5 %all-reduce.4.cloned.1.call-start = ((), (), s32[]{:S(2)}) async-start(), calls=%async_computation.2 | async-start | bytes 262144 | tf_op jit(solution)/shard_map/psum | solution.py:63
  55.7 2.1 copy-start
  56.5 1.3 copy-start.2
  56.5 1.4 copy-start.3
  56.5 1.6 copy-start.4
  59.1 1.3 copy-start.1
  67.6 2.1 copy-start
  68.4 1.3 copy-start.2
  68.4 1.4 copy-start.3
  68.4 1.6 copy-start.4
  71.0 1.3 copy-start.1
  79.5 2.1 copy-start
  80.3 1.3 copy-start.2
  80.4 1.4 copy-start.3
  80.4 1.6 copy-start.4
  82.9 1.3 copy-start.1
  91.5 2.1 copy-start
  92.3 1.3 copy-start.2
  92.3 1.4 copy-start.3
  92.3 1.6 copy-start.4
  94.8 1.3 copy-start.1
  103.4 2.1 copy-start
  104.2 1.3 copy-start.2
  104.2 1.4 copy-start.3
  104.2 1.6 copy-start.4
  106.8 1.3 copy-start.1
  115.3 2.1 copy-start
  116.1 1.3 copy-start.2
  116.1 1.4 copy-start.3
  116.1 1.6 copy-start.4
  118.7 1.3 copy-start.1
  127.2 2.1 copy-start
  128.0 1.3 copy-start.2
  128.1 1.4 copy-start.3
  128.1 1.6 copy-start.4
  130.6 1.3 copy-start.1
  139.2 2.1 copy-start
  140.0 1.3 copy-start.2
  140.0 1.4 copy-start.3
  140.0 1.6 copy-start.4
  142.5 1.3 copy-start.1
  151.1 2.1 copy-start
  151.9 1.3 copy-start.2
  151.9 1.4 copy-start.3
  151.9 1.6 copy-start.4
  154.5 1.3 copy-start.1
  163.0 2.1 copy-start
  163.8 1.3 copy-start.2
  163.8 1.4 copy-start.3
  163.8 1.6 copy-start.4
  166.4 1.3 copy-start.1
  174.9 2.1 copy-start
  175.8 1.4 copy-start.3
  175.8 1.6 copy-start.4
  178.3 1.3 copy-start.1
  186.9 2.1 copy-start
  187.7 1.4 copy-start.3
  187.7 1.6 copy-start.4
  190.3 1.3 copy-start.1
  193.4 102.8 %copy-start.5 = (f32[512,1024]{1,0:T(8,128)}, f32[512,1024]{1,0:T(8,128)S(1)}, u32[]{:S(2)}) copy-start(f32[512,1024]{1,0:T(8,128)S(1)} %broadcast_multiply_fusion) | copy-start | bytes 6291460
  197.4 95.0 %all-gather.8.cloned.1.call-start = ((), (), s32[]{:S(2)}) async-start(), calls=%async_computation.3 | async-start | bytes 1179648 | tf_op jit(solution)/shard_map/all_gather | solution.py:68
  270.1 60.9 %all-reduce.6.cloned.1.call-start = ((), (), s32[]{:S(2)}) async-start(), calls=%async_computation.4 | async-start | bytes 262144 | tf_op jit(solution)/shard_map/psum | solution.py:63
  (2 other events, 2.6 us)
Sparse Core Ops, SparseCore 0:
  9.9 30.4 all-gather.3
  42.3 23.3 all-gather.5
  197.5 34.6 all-reduce.3
  270.2 22.1 all-gather.7
  296.3 34.6 all-reduce.5
where the time goes:
time: 378 us; the launch traced here: 375 us
  waiting for transfers between devices  112 us (30%)
  other arithmetic  102 us (27%)
  blocking collectives  54.6 us (14%)
  local copies, waits for them, and re-layouts  39.1 us (10%)
  loops' own time  26.2 us (7%)
  matrix products  26 us (7%)
  between operations  14.5 us (4%)
    psum x2, waiting for transfers between devices, per_device(): mapped = lax.psum(column_terms, 'shift')  69.5 us
    psum x2, blocking collectives, per_device(): gram_matrix = lax.psum(local_gram, 'row')  44.7 us
    sub x24, other arithmetic, make_some(): difference = window - mirror  28.7 us
    another operation x1, loops' own time, per_device(): lax.fori_loop(0, every_offset.shape[0], add_block, jnp.zeros((block_rows,...  26.2 us
    convert_element_type x24, other arithmetic, make_some(): lax.dynamic_slice_in_dim(extended, offset + M - start - count, count, 0)  26 us
    all_gather x1, waiting for transfers between devices, per_device(): basis_rows = lax.all_gather(own_basis, 'row', axis=1, tiled=True)  22.3 us
    while x120, local copies, waits for them, and re-layouts  19.4 us
    all_gather x1, waiting for transfers between devices, per_device(): gathered = lax.all_gather(snapshots, 'row', axis=0, tiled=True)  19 us
  transfers between devices with their start and end apart: 5, of which 4 were waited for; matrix products, arithmetic and copies ran while one was open for 29% of the time, Pallas kernels for 0%

commit v1 on v0

--- a/solution.py
+++ b/solution.py
@@ -60,7 +60,7 @@
         column_terms = lax.dot_general(
             basis_cols, cov_out, (((1,), (1,)), ((), ())), precision=lax.Precision.HIGHEST
         )
-        mapped = lax.psum(column_terms, "shift")
+        mapped = jnp.sum(jax.lax.all_gather(column_terms, "shift"), 0)
         local_gram = jnp.dot(mapped, mapped.T, precision=lax.Precision.HIGHEST)
         gram_matrix = lax.psum(local_gram, "row")
         own_basis = jnp.dot(factor(gram_matrix), mapped, precision=lax.Precision.HIGHEST)

time: 378 us -> 337 us (0.89)
  waiting for transfers between devices: 112 us -> 44.3 us
  blocking collectives: 54.6 us -> 86.7 us
  matrix products: 26 us -> 20.9 us
    psum x2 -> x0, waiting for transfers between devices: 69.5 us -> none  [per_device(): mapped = lax.psum(column_terms, 'shift')]
    all_gather x0 -> x2, blocking collectives: none -> 32 us  [per_device(): mapped = jnp.sum(jax.lax.all_gather(column_terms, 'shift'), 0)]
  transfers between devices with their start and end apart: 5 -> 3, of which waited for: 4 -> 2; matrix products, arithmetic and copies ran while one was open for 29% -> 33% of each run, Pallas kernels for 0% -> 0%
where the time goes in v1:
time: 337 us; the launch traced here: 334 us
  other arithmetic  102 us (30%)
  blocking collectives  86.7 us (26%)
  waiting for transfers between devices  44.3 us (13%)
  local copies, waits for them, and re-layouts  39.1 us (12%)
  loops' own time  26.2 us (8%)
  matrix products  20.9 us (6%)
  between operations  14.5 us (4%)
    psum x2, blocking collectives, per_device(): gram_matrix = lax.psum(local_gram, 'row')  44.7 us
    all_gather x2, blocking collectives, per_device(): mapped = jnp.sum(jax.lax.all_gather(column_terms, 'shift'), 0)  32 us
    sub x24, other arithmetic, make_some(): difference = window - mirror  28.7 us
    another operation x1, loops' own time, per_device(): lax.fori_loop(0, every_offset.shape[0], add_block, jnp.zeros((block_rows,...  26.2 us
    convert_element_type x24, other arithmetic, make_some(): lax.dynamic_slice_in_dim(extended, offset + M - start - count, count, 0)  26 us
    all_gather x1, waiting for transfers between devices, per_device(): basis_rows = lax.all_gather(own_basis, 'row', axis=1, tiled=True)  23.9 us
    while x120, local copies, waits for them, and re-layouts  19.4 us
    all_gather x1, waiting for transfers between devices, per_device(): gathered = lax.all_gather(snapshots, 'row', axis=0, tiled=True)  19 us
  transfers between devices with their start and end apart: 3, of which 2 were waited for; matrix products, arithmetic and copies ran while one was open for 33% of the time, Pallas kernels for 0%

profile of v1, /device:TPU:0, one launch (start us, length us, event | category | flops | bytes accessed | tf_op | source)
XLA Modules:
  0.0 334.3 jit_solution(10712000800947193462)
XLA Ops:
  8.7 1.3 dynamic-slice
  11.5 9.9 %all-reduce = s32[12]{0:T(128)S(1)} all-reduce(s32[12]{0:T(128)S(1)} %dynamic-update-slice.2), channel_id=1, replica_groups=mesh['row'=8,'shift'=4] {'shift'}, use_global_device_ids=true, to_apply=%add | all-reduce | flops 12 | bytes 96
  21.4 19.0 %all-gather.6.cloned.1.call-done = bf16[4096,2,128]{2,1,0:T(2,128)(2,1)} async-done(((bf16[512,2,128]{2,1,0:T(2,128)(2,1)}), bf16[4096,2,128]{2,1,0:T(2,128)(2,1)}) %all-gather.6.cloned.1.call-update) | async-done | bytes 2097168 | tf_op jit(solution)/shard_map/all_gather | solution.py:38
  40.4 6.4 %pad_maximum_fusion = bf16[4224,2,128]{2,1,0:T(2,128)(2,1)S(1)} fusion(bf16[128,2,128]{2,1,0:T(2,128)(2,1)} %param.10, bf16[4096,2,128]{2,1,0:T(2,128)(2,1)} %all-gather.6.cloned.1.call-done), kind=kLoop, calls=%fused_computation.31 | loop fusion | flops 1081344 | bytes 4325376 | tf_op jit(solution)/shard_map/concatenate | solution.py:39
  46.8 1.6 copy.30
  48.4 143.1 %while.18 = (s32[]{:T(128)}, f32[512,1024]{1,0:T(8,128)}, s32[]{:T(128)}, s32[12]{0:T(128)S(1)}, bf16[4224,2,128]{2,0,1:T(8,128)(2,1)}, /*index=5*/s32[]{:T(128)...) while((s32[]{:T(128)}, f32[512,1024]{1,0:T(8,128)}, ...), condition=%wide.region_1.2_spmd.clone, body=%wide.region_0.1_spmd.clone.sunk | while | flops 273222688 | bytes 47713820 | solution.py:52
  49.7 1.2 dynamic-slice_convert_fusion.4
  52.0 1.2 convert_subtract_fusion.4
  53.2 1.2 slice_bitcast_fusion.8
  56.5 1.2 convert_subtract_fusion.5
  59.1 1.3 copy-done.1
  63.9 1.2 convert_subtract_fusion.4
  65.2 1.2 slice_bitcast_fusion.8
  68.4 1.2 convert_subtract_fusion.5
  71.0 1.3 copy-done.1
  75.8 1.2 convert_subtract_fusion.4
  77.1 1.2 slice_bitcast_fusion.8
  80.4 1.2 convert_subtract_fusion.5
  82.9 1.3 copy-done.1
  87.8 1.2 convert_subtract_fusion.4
  89.0 1.2 slice_bitcast_fusion.8
  92.3 1.2 convert_subtract_fusion.5
  94.9 1.3 copy-done.1
  99.7 1.2 convert_subtract_fusion.4
  100.9 1.2 slice_bitcast_fusion.8
  104.2 1.2 convert_subtract_fusion.5
  106.8 1.3 copy-done.1
  111.6 1.2 convert_subtract_fusion.4
  112.9 1.2 slice_bitcast_fusion.8
  116.1 1.2 convert_subtract_fusion.5
  118.7 1.3 copy-done.1
  123.5 1.2 convert_subtract_fusion.4
  124.8 1.2 slice_bitcast_fusion.8
  128.1 1.2 convert_subtract_fusion.5
  130.6 1.3 copy-done.1
  135.5 1.2 convert_subtract_fusion.4
  136.7 1.2 slice_bitcast_fusion.8
  140.0 1.2 convert_subtract_fusion.5
  142.6 1.3 copy-done.1
  147.4 1.2 convert_subtract_fusion.4
  148.6 1.2 slice_bitcast_fusion.8
  151.9 1.2 convert_subtract_fusion.5
  154.5 1.3 copy-done.1
  159.3 1.2 convert_subtract_fusion.4
  160.6 1.2 slice_bitcast_fusion.8
  166.4 1.3 copy-done.1
  171.2 1.2 convert_subtract_fusion.4
  172.5 1.2 slice_bitcast_fusion.8
  178.3 1.3 copy-done.1
  183.2 1.2 convert_subtract_fusion.4
  184.4 1.2 slice_bitcast_fusion.8
  190.3 1.3 copy-done.1
  191.6 1.8 broadcast_multiply_fusion
  193.4 3.3 fusion.16
  196.7 16.0 %all-gather = f32[256,512]{1,0:T(8,128)S(1)} all-gather(f32[64,512]{1,0:T(8,128)S(1)} %fusion.16), channel_id=2, replica_groups=mesh['row'=8,'shift'=4] {'shift'}, dimensions={0}, use_global_device_ids=true | all-gather | bytes 655360 | tf_op jit(solution)/shard_map/all_gather | solution.py:63
  213.1 22.4 %psum.14 = f32[64,64]{0,1:T(8,128)S(1)} all-reduce(f32[64,64]{0,1:T(8,128)S(1)} %fusion.32), channel_id=1, replica_groups=mesh['row'=8,'shift'=4] {'row'}, use_global_device_ids=true, to_apply=%region_3.4 | all-reduce | flops 4096 | bytes 32768 | tf_op jit(solution)/shard_map/psum | solution.py:65
  235.5 5.8 %cholesky.44 = f32[64,64]{1,0:T(8,128)S(1)} custom-call(f32[64,64]{1,0:T(8,128)S(1)} %fusion.27), custom_call_target="Cholesky" | custom-call | tf_op jit(solution)/shard_map/jit(cholesky)/cholesky | solution.py:27
  242.7 4.9 %custom-call.7 = f32[1,64,64]{1,2,0:T(8,128)S(1)} custom-call(f32[1,64,64]{2,1,0:T(8,128)S(1)} %fusion.22), custom_call_target="InvertDiagBlocksLowerTriangular" | custom-call | tf_op jit(solution)/shard_map/jit(_solve_triangular)/triangular_solve | solution.py:29
  248.8 23.9 %all-gather.10.cloned.1.call-done = f32[64,4096]{1,0:T(8,128)} async-done(((f32[64,512]{1,0:T(8,128)}), f32[64,4096]{1,0:T(8,128)}) %all-gather.10.cloned.1.call-update) | async-done | bytes 1048592 | tf_op jit(solution)/shard_map/all_gather | solution.py:68
  272.7 3.1 fusion.14
  275.8 16.0 %all-gather.1 = f32[256,512]{1,0:T(8,128)S(1)} all-gather(f32[64,512]{1,0:T(8,128)S(1)} %fusion.14), channel_id=3, replica_groups=mesh['row'=8,'shift'=4] {'shift'}, dimensions={0}, use_global_device_ids=true | all-gather | bytes 655360 | tf_op jit(solution)/shard_map/all_gather | solution.py:63
  292.1 22.4 %psum.15 = f32[64,64]{0,1:T(8,128)S(1)} all-reduce(f32[64,64]{0,1:T(8,128)S(1)} %fusion.34), channel_id=1, replica_groups=mesh['row'=8,'shift'=4] {'row'}, use_global_device_ids=true, to_apply=%region_7.10 | all-reduce | flops 4096 | bytes 32768 | tf_op jit(solution)/shard_map/psum | solution.py:65
  314.5 5.8 %cholesky.55 = f32[64,64]{1,0:T(8,128)S(1)} custom-call(f32[64,64]{1,0:T(8,128)S(1)} %fusion.25), custom_call_target="Cholesky" | custom-call | tf_op jit(solution)/shard_map/jit(cholesky)/cholesky | solution.py:27
  321.7 4.9 %custom-call.8 = f32[1,64,64]{1,2,0:T(8,128)S(1)} custom-call(f32[1,64,64]{2,1,0:T(8,128)S(1)} %fusion.23), custom_call_target="InvertDiagBlocksLowerTriangular" | custom-call | tf_op jit(solution)/shard_map/jit(_solve_triangular)/triangular_solve | solution.py:29
  (248 shorter events, 68.7 us)
Async XLA Ops:
  7.2 33.2 %all-gather.6.cloned.1.call-start = ((), (), s32[]{:S(2)}) async-start(), calls=%async_computation | async-start | bytes 2359296 | tf_op jit(solution)/shard_map/all_gather | solution.py:38
  7.9 185.5 %all-gather.8.cloned.1.call-start = ((), (), s32[]{:S(2)}) async-start(), calls=%async_computation.1 | async-start | bytes 1179648 | tf_op jit(solution)/shard_map/all_gather | solution.py:56
  8.6 264.0 %all-gather.10.cloned.1.call-start = ((), (), s32[]{:S(2)}) async-start(), calls=%async_computation.2 | async-start | bytes 1179648 | tf_op jit(solution)/shard_map/all_gather | solution.py:68
  55.7 2.1 copy-start
  56.5 1.3 copy-start.2
  56.5 1.4 copy-start.3
  56.5 1.6 copy-start.4
  59.1 1.3 copy-start.1
  67.6 2.1 copy-start
  68.4 1.3 copy-start.2
  68.4 1.4 copy-start.3
  68.4 1.6 copy-start.4
  71.0 1.3 copy-start.1
  79.5 2.1 copy-start
  80.3 1.3 copy-start.2
  80.4 1.4 copy-start.3
  80.4 1.6 copy-start.4
  82.9 1.3 copy-start.1
  91.5 2.1 copy-start
  92.3 1.3 copy-start.2
  92.3 1.4 copy-start.3
  92.3 1.6 copy-start.4
  94.8 1.3 copy-start.1
  103.4 2.1 copy-start
  104.2 1.3 copy-start.2
  104.2 1.4 copy-start.3
  104.2 1.6 copy-start.4
  106.8 1.3 copy-start.1
  115.3 2.1 copy-start
  116.1 1.3 copy-start.2
  116.1 1.4 copy-start.3
  116.1 1.6 copy-start.4
  118.7 1.3 copy-start.1
  127.2 2.1 copy-start
  128.0 1.3 copy-start.2
  128.1 1.4 copy-start.3
  128.1 1.6 copy-start.4
  130.6 1.3 copy-start.1
  139.2 2.1 copy-start
  140.0 1.3 copy-start.2
  140.0 1.4 copy-start.3
  140.0 1.6 copy-start.4
  142.5 1.3 copy-start.1
  151.1 2.1 copy-start
  151.9 1.3 copy-start.2
  151.9 1.4 copy-start.3
  151.9 1.6 copy-start.4
  154.5 1.3 copy-start.1
  163.0 2.1 copy-start
  163.8 1.3 copy-start.2
  163.8 1.4 copy-start.3
  163.8 1.6 copy-start.4
  166.4 1.3 copy-start.1
  174.9 2.1 copy-start
  175.7 1.3 copy-start.2
  175.8 1.4 copy-start.3
  175.8 1.6 copy-start.4
  178.3 1.3 copy-start.1
  186.9 2.1 copy-start
  187.7 1.3 copy-start.2
  187.7 1.4 copy-start.3
  187.7 1.6 copy-start.4
  190.3 1.3 copy-start.1
  193.4 79.3 %copy-start.5 = (f32[512,1024]{1,0:T(8,128)}, f32[512,1024]{1,0:T(8,128)S(1)}, u32[]{:S(2)}) copy-start(f32[512,1024]{1,0:T(8,128)S(1)} %broadcast_multiply_fusion) | copy-start | bytes 6291460
Sparse Core Ops, SparseCore 0:
  9.9 30.4 all-gather.5
  42.3 23.3 all-gather.7
  248.9 23.7 all-gather.9
